TPU v7x, 512 devices: a 8x2x16 block of a 8x16x16 slice. The times are simulated.
512 devices in a mesh: rep: 2 (over y), blk: 128 (over z, x), head: 2 (over core).
Axes of the slice: x: 8, y: 2, z: 16, core: 2. Of those that a mesh axis runs over, the one named last changes fastest.
The devices are a block of a 8x16x16 slice.
Arguments:
- queries: bfloat16 [2, 8192, 8192], P('rep', 'blk', 'head'), parts along dimension 0, may hold values from -200 to 200
- keys: bfloat16 [2, 8192, 512], P('rep', 'blk', 'head'), parts along dimension 0, may hold values from -6 to 6
- values: bfloat16 [2, 8192, 512], P('rep', 'blk', 'head'), parts along dimension 0, may hold values from -6 to 6
- prompt_length: int32 [2], P('rep'), parts along dimension 0, may hold values from 4096 to 8192
- span_order: int32 [512], P('rep'), parts along dimension 0, may hold values from 0 to 255, as said below
Outputs:
- attended: bfloat16 [2, 8192, 8192], P('rep', 'blk', 'head'), parts along dimension 0
There are 2 independent parts, one for each index of `rep`. A program takes and returns all parts, laid end to end along the dimension named above; each array names one. Nothing has to cross between parts.
Inputs may be any that keep to these rules, and one draw needn't show every extreme that they name: `span_order`: each of the 256 span numbers stands in exactly one slot.
All inputs are finite; a program needn't handle non-finite values.
Results may differ from a plain program's by a relative error of at most 0.0065.
Values may be sent and summed in bfloat16 or wider, within the bound.
No kernel may reach another device: no remote copies, remote signals or barrier semaphores. Data moves between devices by JAX's collectives and lax.ppermute only.
A program may use at most 64 MiB of HBM per device.

v0:
```python
import jax
import jax.numpy as jnp
from jax import lax
from jax.experimental import pallas as pl
from jax.experimental.pallas import tpu as pltpu
from jax.sharding import Mesh
from jax.sharding import PartitionSpec as P

HEAD_WIDTH = 128
BLK = ("blk_0", "blk_1")
BLOCK_SPANS = 16
STEP_BLOCKS = (8, 4, 2, 1)
NEG_FILL = -1e30
LOG2_E = 1.4426950408889634
SENT_SCALE = 4096.0


def attend(span_order, prompt_length, q, gathered, group, span, first, away):
    spans = gathered.shape[0] // 2
    deep, lines = lax.axis_size("blk_0"), lax.axis_size("blk_1")
    blocks = spans // BLOCK_SPANS
    keys_of = BLOCK_SPANS * span
    rows = group * span
    factor = LOG2_E * HEAD_WIDTH ** (-0.5) / SENT_SCALE

    def kernel(order_ref, length_ref, q_ref, kv_ref, o_ref, kept_ref, held_ref, s_buf, q_buf, m_buf, acc_buf):
        limit = length_ref[0]
        place_on = {name: lax.axis_index(name) for name in BLK}
        if away:
            place_on[first] = place_on[first] + 1 - 2 * (place_on[first] % 2)
        device = place_on["blk_0"] * lines + place_on["blk_1"]
        depth_step, line_step = (4, 4 * deep) if first == "blk_0" else (4 * lines, 4)

        def note(i, _):
            for u in range(2 * lines):
                held_ref[order_ref[i * (2 * lines) + u]] = u // 2 * line_step + i * depth_step + u % 2
            return 0

        lax.fori_loop(0, deep, note, 0)

        def block(b, which):
            parts = [kv_ref[held_ref[b * BLOCK_SPANS + i] + 2 * which] for i in range(BLOCK_SPANS)]
            return jnp.concatenate(parts, axis=0)

        def tile(which, _):
            place = order_ref[2 * device + which]
            count = jnp.where(place * span < limit, place // BLOCK_SPANS + 1, 0)
            row0 = pl.multiple_of(which * span, span)

            @pl.when(count == 0)
            def _():
                o_ref[pl.ds(row0, span), :] = jnp.zeros((span, group * HEAD_WIDTH), o_ref.dtype)

            @pl.when(count > 0)
            def _():
                for g in range(group):
                    q_buf[g * span : (g + 1) * span, :] = q_ref[
                        pl.ds(row0, span), g * HEAD_WIDTH : (g + 1) * HEAD_WIDTH
                    ]
                m_buf[...] = jnp.full(m_buf.shape, NEG_FILL, jnp.float32)
                acc_buf[...] = jnp.zeros(acc_buf.shape, jnp.float32)

                def score(first, size):
                    top = m_buf[...]
                    for u in range(size):
                        s = lax.dot_general(
                            q_buf[...],
                            block(first + u, 0),
                            (((1,), (1,)), ((), ())),
                            preferred_element_type=jnp.float32,
                        )
                        gap = place * span - (first + u) * keys_of
                        key = lax.broadcasted_iota(jnp.int32, (span, keys_of), 1)
                        row = lax.broadcasted_iota(jnp.int32, (span, keys_of), 0) + gap
                        s = jnp.where((key <= row)[None], s.reshape(group, span, keys_of), NEG_FILL)
                        s = s.reshape(rows, keys_of)
                        s_buf[first + u] = s
                        for c in range(keys_of // 128):
                            top = jnp.maximum(top, s[:, c * 128 : (c + 1) * 128])
                    m_buf[...] = top

                def mix(first, size):
                    top = jnp.concatenate([m_buf[...]] * (keys_of // 128), axis=1)
                    total = acc_buf[...]
                    for u in range(size):
                        w = jnp.exp2((s_buf[first + u] - top) * factor).astype(jnp.bfloat16)
                        v = block(first + u, 1)
                        wide = jnp.concatenate([v, jnp.ones_like(v)], axis=1)
                        total += jnp.dot(w, wide, preferred_element_type=jnp.float32)
                    acc_buf[...] = total


                def in_steps(work):
                    done = 0
                    for size in STEP_BLOCKS:
                        times = (count - done) // size

                        def step(i, _, done=done, size=size):
                            work(done + i * size, size)
                            return 0

                        lax.fori_loop(0, times, step, 0)
                        done = done + times * size

                in_steps(score)
                m_buf[...] = jnp.broadcast_to(jnp.max(m_buf[...], axis=1, keepdims=True), m_buf.shape)
                in_steps(mix)
                out = acc_buf[:, :HEAD_WIDTH] / (acc_buf[:, HEAD_WIDTH:] * SENT_SCALE)
                row_pos = place * span + lax.broadcasted_iota(jnp.int32, out.shape, 0) % span
                out = jnp.where(row_pos < limit, out, 0.0).astype(o_ref.dtype)
                for g in range(group):
                    o_ref[pl.ds(row0, span), g * HEAD_WIDTH : (g + 1) * HEAD_WIDTH] = out[
                        g * span : (g + 1) * span
                    ]

            return 0

        lax.fori_loop(0, 2, tile, 0)

    return pl.pallas_call(
        kernel,
        out_shape=(
            jax.ShapeDtypeStruct(q.shape, q.dtype),
            jax.ShapeDtypeStruct(gathered.shape, gathered.dtype),
        ),
        in_specs=[
            pl.BlockSpec(memory_space=pltpu.SMEM),
            pl.BlockSpec(memory_space=pltpu.SMEM),
            pl.BlockSpec(memory_space=pltpu.VMEM),
            pl.BlockSpec(memory_space=pltpu.VMEM),
        ],
        out_specs=(pl.BlockSpec(memory_space=pltpu.VMEM), pl.BlockSpec(memory_space=pltpu.VMEM)),
        input_output_aliases={3: 1},
        scratch_shapes=[
            pltpu.SMEM((spans,), jnp.int32),
            pltpu.VMEM((blocks, rows, keys_of), jnp.float32),
            pltpu.VMEM((rows, HEAD_WIDTH), jnp.bfloat16),
            pltpu.VMEM((rows, 128), jnp.float32),
            pltpu.VMEM((rows, 2 * HEAD_WIDTH), jnp.float32),
        ],
        compiler_params=pltpu.CompilerParams(vmem_limit_bytes=32 * 1024 * 1024),
    )(span_order, prompt_length, q, gathered)


def work(first, then):
    def run(queries, keys, values, prompt_length, span_order):
        half = lax.axis_index(first) % 2
        tok_rows = queries.shape[1]
        span = tok_rows // 2
        local_heads = keys.shape[2] // HEAD_WIDTH
        group = queries.shape[2] // (local_heads * HEAD_WIDTH)
        width = group * HEAD_WIDTH
        swap = [(i, i ^ 1) for i in range(lax.axis_size(first))]

        own_q = lax.dynamic_slice_in_dim(queries[0], half * width, width, 1)
        their_q = lax.ppermute(
            lax.dynamic_slice_in_dim(queries[0], (1 - half) * width, width, 1), first, swap
        )

        pieces = [
            x[0, :, h * HEAD_WIDTH : (h + 1) * HEAD_WIDTH] for h in range(local_heads) for x in (keys, values)
        ]
        packed = (jnp.stack(pieces).astype(jnp.float32) * SENT_SCALE).astype(jnp.float16)
        part = lax.all_gather(packed, first, axis=0, tiled=False)
        part = part.reshape(-1, local_heads, 2, tok_rows, HEAD_WIDTH)
        part = lax.dynamic_index_in_dim(part, half, 1, keepdims=False)

        low = half == 0
        part, own_q, low = lax.optimization_barrier((part, own_q, low))
        gathered = lax.all_gather(part, then, axis=0, tiled=False).astype(jnp.bfloat16)
        gathered = gathered.reshape(-1, span, HEAD_WIDTH)
        theirs, gathered = attend(span_order, prompt_length, their_q, gathered, group, span, first, True)
        other = lax.ppermute(theirs, first, swap)
        own, _ = attend(span_order, prompt_length, own_q, gathered, group, span, first, False)
        left = jnp.where(low, own, other)
        right = jnp.where(low, other, own)
        return jnp.concatenate([left, right], axis=1)[None]

    return run


def shards(queries, keys, values, prompt_length, span_order):
    return lax.cond(
        lax.axis_index("head") == 0,
        work("blk_0", "blk_1"),
        work("blk_1", "blk_0"),
        queries,
        keys,
        values,
        prompt_length,
        span_order,
    )


def solution(mesh):
    blk = mesh.shape["blk"]
    split = Mesh(
        mesh.devices.reshape(mesh.shape["rep"], blk // 8, 8, mesh.shape["head"]),
        ("rep", "blk_0", "blk_1", "head"),
    )
    in_specs = (
        P("rep", BLK, "head"),
        P("rep", BLK, "head"),
        P("rep", BLK, "head"),
        P("rep"),
        P("rep"),
    )
    out_specs = P("rep", BLK, "head")
    return jax.shard_map(
        shards, mesh=split, in_specs=in_specs, out_specs=out_specs, check_vma=False
    )
```

profile of v0, /device:TPU:80, one launch (start us, length us, event | category | flops | bytes accessed | tf_op | source)
XLA Modules:
  0.0 131.4 jit_solution(11974008961413544491)
XLA Ops:
  0.0 130.6 %conditional.1 = (bf16[1,64,4096]{2,1,0:T(8,128)(2,1)S(1)}) conditional(s32[]{:T(128)} %convert_element_type.49, (bf16[1,64,256]{2,1,0:T(8,128)(2,1)}, bf16[1,64,256]{2,1,0:T(8,128)(2,1)}, bf16[1,64,4096]{2,1,0:T(8,128)(2,1)}, s32[256]{0:T(256)}, s32[1]{0:T(128)}) %tuple.13, (bf16[1,64,256]{2,1,0:T(8,128)(2,1)}, bf16[1,64,256]{2,1,0:T(8,128)(2,1)}, ...), branch_computations={%region_0.1_spmd, %region_1.2_spmd} | conditional | flops 3604507 | bytes 20779424 | solution.py:183
  0.0 1.1 dynamic-slice_bitcast_fusion.5
  1.1 6.0 %collective-permute-start.2 = (bf16[64,2048]{1,0:T(8,128)(2,1)S(1)}, bf16[64,2048]{1,0:T(8,128)(2,1)S(1)}, u32[]{:S(2)}, u32[]{:S(2)}) collective-permute-start(bf16[64,2048]{1,0:T(8,128)(2,1)S(1)} %get-tuple-element.64), channel_id=1, source_target_pairs={{0,16},{16,0},{32,48},{48,32},{64,80},{80,64},{96,112},{112,96},{1... | collective-permute-start | bytes 786440 | tf_op jit(solution)/shard_map/cond/branch_1_fun/ppermute | solution.py:156
  7.1 0.8 slice_bitcast_fusion.6
  7.9 70.9 %all-gather.6 = f16[16,4,64,128]{3,2,1,0:T(8,128)(2,1)S(1)} all-gather(f16[1,4,64,128]{3,2,1,0:T(8,128)(2,1)S(1)} %multiply_convert_fusion.1), channel_id=1, replica_groups=mesh['rep'=2,'blk_0'=16,'blk_1'=8,'head'=2] {'blk_0'}, dimensions={0}, use_global_device_ids=true | all-gather | bytes 1114112 | tf_op jit(solution)/shard_map/cond/branch_1_fun/all_gather | solution.py:164
  78.8 0.2 dynamic-slice_bitcast_fusion.3
  79.0 33.5 %all-gather.7 = f16[128,2,64,128]{3,2,1,0:T(8,128)(2,1)S(1)} all-gather(f16[16,2,64,128]{3,2,1,0:T(8,128)(2,1)S(1)} %dynamic-slice_bitcast_fusion.3), channel_id=3, replica_groups=mesh['rep'=2,'blk_0'=16,'blk_1'=8,'head'=2] {'blk_1'}, dimensions={0}, use_global_device_ids=true | all-gather | bytes 4718592 | tf_op jit(solution)/shard_map/cond/branch_1_fun/all_gather | solution.py:170
  112.4 0.0 copy-start.2
  112.5 1.9 %convert_element_type.51 = bf16[128,2,64,128]{3,2,1,0:T(8,128)(2,1)S(1)} convert(f16[128,2,64,128]{3,2,1,0:T(8,128)(2,1)S(1)} %all-gather.7) | non-fusion elementwise | flops 2097152 | bytes 8388608 | tf_op jit(solution)/shard_map/cond/branch_1_fun/convert_element_type | solution.py:170
  114.4 0.0 collective-permute-done.2.q_ref
  114.4 0.0 copy-done.2
  114.4 7.0 %branch_1_fun.2 = (bf16[64,2048]{1,0:T(8,128)(2,1)S(1)}, bf16[512,32,128]{2,1,0:T(8,128)(2,1)S(1)}) custom-call(s32[256]{0:T(256)S(1)} %copy-done.2, s32[1]{0:T(128)} %get-tuple-element.44.length_ref, bf16[64,2048]{1,0:T(8,128)(2,1)S(1)} %collective-permute-done.2.q_ref, bf16[512,32,128]{2,1,0:T(8,128)(2,1)S(1)} %bitcast.37), custom_call_target="tpu_custom_call", output_to_operand_aliasing={{1}: (3, {})} | custom-call | tf_op jit(solution)/shard_map/cond/branch_1_fun/pallas_call | solution.py:120
  121.4 2.4 %collective-permute-start.3 = (bf16[64,2048]{1,0:T(8,128)(2,1)S(1)}, bf16[64,2048]{1,0:T(8,128)(2,1)S(1)}, u32[]{:S(2)}, u32[]{:S(2)}) collective-permute-start(bf16[64,2048]{1,0:T(8,128)(2,1)S(1)} %get-tuple-element.49), channel_id=1, source_target_pairs={{0,16},{16,0},{32,48},{48,32},{64,80},{80,64},{96,112},{112,96},{1... | collective-permute-start | bytes 786440 | tf_op jit(solution)/shard_map/cond/branch_1_fun/ppermute | solution.py:173
  123.8 6.4 %branch_1_fun.3 = (bf16[64,2048]{1,0:T(8,128)(2,1)S(1)}, bf16[512,32,128]{2,1,0:T(8,128)(2,1)S(1)}) custom-call(s32[256]{0:T(256)S(1)} %copy-done.2, s32[1]{0:T(128)} %get-tuple-element.44.length_ref, bf16[64,2048]{1,0:T(8,128)(2,1)S(1)} %get-tuple-element.45.q_ref, bf16[512,32,128]{2,1,0:T(8,128)(2,1)S(1)} %get-tuple-element.47.kv_ref), custom_call_target="tpu_custom_call", output_to_operand_aliasing={{1}: (3, {})} | custom-call | tf_op jit(solution)/shard_map/cond/branch_1_fun/pallas_call | solution.py:120
  130.2 0.0 collective-permute-done.3
  130.6 0.0 copy-start
  130.6 0.8 copy-done
  (3 shorter events, 0.1 us)
Async XLA Ops:
  1.1 113.3 %collective-permute-start.2 = (bf16[64,2048]{1,0:T(8,128)(2,1)S(1)}, bf16[64,2048]{1,0:T(8,128)(2,1)S(1)}, u32[]{:S(2)}, u32[]{:S(2)}) collective-permute-start(bf16[64,2048]{1,0:T(8,128)(2,1)S(1)} %get-tuple-element.64), channel_id=1, source_target_pairs={{0,16},{16,0},{32,48},{48,32},{64,80},{80,64},{96,112},{112,96},{1... | collective-permute-start | bytes 786440 | tf_op jit(solution)/shard_map/cond/branch_1_fun/ppermute | solution.py:156
  112.4 2.0 %copy-start.2 = (s32[256]{0:T(256)S(1)}, s32[256]{0:T(256)}, u32[]{:S(2)}) copy-start(s32[256]{0:T(256)} %get-tuple-element.43.order_ref) | copy-start | bytes 3076 | tf_op jit(solution)/shard_map/cond
  121.4 8.8 %collective-permute-start.3 = (bf16[64,2048]{1,0:T(8,128)(2,1)S(1)}, bf16[64,2048]{1,0:T(8,128)(2,1)S(1)}, u32[]{:S(2)}, u32[]{:S(2)}) collective-permute-start(bf16[64,2048]{1,0:T(8,128)(2,1)S(1)} %get-tuple-element.49), channel_id=1, source_target_pairs={{0,16},{16,0},{32,48},{48,32},{64,80},{80,64},{96,112},{112,96},{1... | collective-permute-start | bytes 786440 | tf_op jit(solution)/shard_map/cond/branch_1_fun/ppermute | solution.py:173
  130.6 0.8 copy-start
where the time goes:
time: 133 us; the launch traced here: 131 us
  blocking collectives  104 us (78%)
  Pallas kernels  13.4 us (10%)
  starting transfers between devices  8.39 us (6%)
  local copies, waits for them, and re-layouts  2.8 us (2%)
  other arithmetic  2.05 us (2%)
    all_gather x1, blocking collectives, run(): part = lax.all_gather(packed, first, axis=0, tiled=False)  70.9 us
    all_gather x1, blocking collectives, run(): lax.all_gather(part, then, axis=0, tiled=False).astype(jnp.bfloat16)  33.5 us
    pallas_call x2, Pallas kernels, attend(): pl.pallas_call(kernel, out_shape=(jax.ShapeDtypeStruct(q.shape, q.dtype),...  13.4 us
    ppermute x1, starting transfers between devices, run(): lax.ppermute(lax.dynamic_slice_in_dim(queries[0], (1 - half) * width, wid...  6.03 us
  transfers between devices with their start and end apart: 2, of which 0 were waited for; matrix products, arithmetic and copies ran while one was open for 2% of the time, Pallas kernels for 5%

commit v1 on v0

--- a/solution.py
+++ b/solution.py
@@ -15,20 +15,35 @@
 SENT_SCALE = 4096.0
 
 
-def attend(span_order, prompt_length, q, gathered, group, span, first, away):
+def attend(span_order, prompt_length, rows_of, gathered, partial, group, span, first):
     spans = gathered.shape[0] // 2
     deep, lines = lax.axis_size("blk_0"), lax.axis_size("blk_1")
     blocks = spans // BLOCK_SPANS
+    opening = partial is None
     keys_of = BLOCK_SPANS * span
     rows = group * span
     factor = LOG2_E * HEAD_WIDTH ** (-0.5) / SENT_SCALE
 
-    def kernel(order_ref, length_ref, q_ref, kv_ref, o_ref, kept_ref, held_ref, s_buf, q_buf, m_buf, acc_buf):
+    def kernel(order_ref, length_ref, *refs):
+        if opening:
+            their_q_ref, own_q_ref, kv_ref, their_o_ref, own_o_ref, kept_ref = refs[:6]
+        else:
+            own_q_ref, kv_ref, partial_ref, own_o_ref, kept_ref = refs[:5]
+        held_ref, s_buf, q_buf, m_buf, acc_buf, o_buf = refs[-6:]
         limit = length_ref[0]
         place_on = {name: lax.axis_index(name) for name in BLK}
-        if away:
-            place_on[first] = place_on[first] + 1 - 2 * (place_on[first] % 2)
-        device = place_on["blk_0"] * lines + place_on["blk_1"]
+        own_device = place_on["blk_0"] * lines + place_on["blk_1"]
+        place_on[first] = place_on[first] + 1 - 2 * (place_on[first] % 2)
+        their_device = place_on["blk_0"] * lines + place_on["blk_1"]
+
+        def blocks_for(device, which):
+            place = order_ref[2 * device + which]
+            return jnp.where(place * span < limit, place // BLOCK_SPANS + 1, 0)
+
+        costs = [blocks_for(own_device, 0), blocks_for(own_device, 1)]
+        ahead = costs[0] + costs[1] - blocks_for(their_device, 0) - blocks_for(their_device, 1)
+        early = jnp.where(jnp.abs(costs[1] - ahead) < jnp.abs(costs[0] - ahead), 1, 0)
+        gain = jnp.abs(jnp.where(early == 1, costs[1], costs[0]) - ahead) < ahead
         depth_step, line_step = (4, 4 * deep) if first == "blk_0" else (4 * lines, 4)
 
         def note(i, _):
@@ -42,21 +57,39 @@
             parts = [kv_ref[held_ref[b * BLOCK_SPANS + i] + 2 * which] for i in range(BLOCK_SPANS)]
             return jnp.concatenate(parts, axis=0)
 
-        def tile(which, _):
+        def tile(t, _):
+            if opening:
+                theirs = t < 2
+                which = jnp.where(theirs, t, early)
+                device = jnp.where(theirs, their_device, own_device)
+            else:
+                theirs = None
+                which = t
+                device = own_device
             place = order_ref[2 * device + which]
             count = jnp.where(place * span < limit, place // BLOCK_SPANS + 1, 0)
             row0 = pl.multiple_of(which * span, span)
 
-            @pl.when(count == 0)
-            def _():
-                o_ref[pl.ds(row0, span), :] = jnp.zeros((span, group * HEAD_WIDTH), o_ref.dtype)
-
-            @pl.when(count > 0)
-            def _():
+            def load(q_ref):
                 for g in range(group):
                     q_buf[g * span : (g + 1) * span, :] = q_ref[
                         pl.ds(row0, span), g * HEAD_WIDTH : (g + 1) * HEAD_WIDTH
                     ]
+
+            def store(o_ref):
+                o_ref[pl.ds(row0, span), :] = o_buf[...]
+
+            @pl.when(count == 0)
+            def _():
+                o_buf[...] = jnp.zeros(o_buf.shape, o_buf.dtype)
+
+            @pl.when(count > 0)
+            def _():
+                if opening:
+                    pl.when(theirs)(lambda: load(their_q_ref))
+                    pl.when(jnp.logical_not(theirs))(lambda: load(own_q_ref))
+                else:
+                    load(own_q_ref)
                 m_buf[...] = jnp.full(m_buf.shape, NEG_FILL, jnp.float32)
                 acc_buf[...] = jnp.zeros(acc_buf.shape, jnp.float32)
 
@@ -107,39 +140,44 @@
                 in_steps(mix)
                 out = acc_buf[:, :HEAD_WIDTH] / (acc_buf[:, HEAD_WIDTH:] * SENT_SCALE)
                 row_pos = place * span + lax.broadcasted_iota(jnp.int32, out.shape, 0) % span
-                out = jnp.where(row_pos < limit, out, 0.0).astype(o_ref.dtype)
+                out = jnp.where(row_pos < limit, out, 0.0).astype(o_buf.dtype)
                 for g in range(group):
-                    o_ref[pl.ds(row0, span), g * HEAD_WIDTH : (g + 1) * HEAD_WIDTH] = out[
-                        g * span : (g + 1) * span
-                    ]
-
+                    o_buf[:, g * HEAD_WIDTH : (g + 1) * HEAD_WIDTH] = out[g * span : (g + 1) * span]
+
+            if opening:
+                pl.when(theirs)(lambda: store(their_o_ref))
+                pl.when(jnp.logical_not(theirs))(lambda: store(own_o_ref))
+            else:
+                store(own_o_ref)
             return 0
 
-        lax.fori_loop(0, 2, tile, 0)
-
+        if opening:
+            lax.fori_loop(0, jnp.where(gain, 3, 2), tile, 0)
+        else:
+            begin = jnp.where(gain & (early == 0), 1, 0)
+            lax.fori_loop(begin, jnp.where(gain & (early == 1), 1, 2), tile, 0)
+
+    vmem = pl.BlockSpec(memory_space=pltpu.VMEM)
+    smem = pl.BlockSpec(memory_space=pltpu.SMEM)
+    rows_shape = jax.ShapeDtypeStruct(rows_of[0].shape, rows_of[0].dtype)
+    operands = [*rows_of, gathered] + ([] if opening else [partial])
+    outs = len(rows_of) + 1
     return pl.pallas_call(
         kernel,
-        out_shape=(
-            jax.ShapeDtypeStruct(q.shape, q.dtype),
-            jax.ShapeDtypeStruct(gathered.shape, gathered.dtype),
-        ),
-        in_specs=[
-            pl.BlockSpec(memory_space=pltpu.SMEM),
-            pl.BlockSpec(memory_space=pltpu.SMEM),
-            pl.BlockSpec(memory_space=pltpu.VMEM),
-            pl.BlockSpec(memory_space=pltpu.VMEM),
-        ],
-        out_specs=(pl.BlockSpec(memory_space=pltpu.VMEM), pl.BlockSpec(memory_space=pltpu.VMEM)),
-        input_output_aliases={3: 1},
+        out_shape=(rows_shape,) * len(rows_of) + (jax.ShapeDtypeStruct(gathered.shape, gathered.dtype),),
+        in_specs=[smem, smem] + [vmem] * len(operands),
+        out_specs=(vmem,) * outs,
+        input_output_aliases={4: 2} if opening else {3: 1, 4: 0},
         scratch_shapes=[
             pltpu.SMEM((spans,), jnp.int32),
             pltpu.VMEM((blocks, rows, keys_of), jnp.float32),
             pltpu.VMEM((rows, HEAD_WIDTH), jnp.bfloat16),
             pltpu.VMEM((rows, 128), jnp.float32),
             pltpu.VMEM((rows, 2 * HEAD_WIDTH), jnp.float32),
+            pltpu.VMEM((span, group * HEAD_WIDTH), jnp.bfloat16),
         ],
         compiler_params=pltpu.CompilerParams(vmem_limit_bytes=32 * 1024 * 1024),
-    )(span_order, prompt_length, q, gathered)
+    )(span_order, prompt_length, *operands)
 
 
 def work(first, then):
@@ -169,9 +207,11 @@
         part, own_q, low = lax.optimization_barrier((part, own_q, low))
         gathered = lax.all_gather(part, then, axis=0, tiled=False).astype(jnp.bfloat16)
         gathered = gathered.reshape(-1, span, HEAD_WIDTH)
-        theirs, gathered = attend(span_order, prompt_length, their_q, gathered, group, span, first, True)
+        theirs, own, gathered = attend(
+            span_order, prompt_length, (their_q, own_q), gathered, None, group, span, first
+        )
         other = lax.ppermute(theirs, first, swap)
-        own, _ = attend(span_order, prompt_length, own_q, gathered, group, span, first, False)
+        own, _ = attend(span_order, prompt_length, (own_q,), gathered, own, group, span, first)
         left = jnp.where(low, own, other)
         right = jnp.where(low, other, own)
         return jnp.concatenate([left, right], axis=1)[None]

time: 133 us -> 132 us (level)
  Pallas kernels: 13.4 us -> 9.72 us
    pallas_call x2, Pallas kernels: 13.4 us -> 9.72 us  [attend(): pl.pallas_call(kernel, out_shape=(rows_shape,) * len(rows_of) + (jax.Shap...]
  transfers between devices with their start and end apart: 2 -> 2, of which waited for: 0 -> 1; matrix products, arithmetic and copies ran while one was open for 2% -> 2% of each run, Pallas kernels for 5% -> 3%
where the time goes in v1:
time: 132 us; the launch traced here: 130 us
  blocking collectives  104 us (79%)
  Pallas kernels  9.72 us (7%)
  starting transfers between devices  9.35 us (7%)
  local copies, waits for them, and re-layouts  2.8 us (2%)
  other arithmetic  2.05 us (2%)
    all_gather x1, blocking collectives, run(): part = lax.all_gather(packed, first, axis=0, tiled=False)  70.9 us
    all_gather x1, blocking collectives, run(): lax.all_gather(part, then, axis=0, tiled=False).astype(jnp.bfloat16)  33.5 us
    pallas_call x2, Pallas kernels, attend(): pl.pallas_call(kernel, out_shape=(rows_shape,) * len(rows_of) + (jax.Shap...  9.72 us
    ppermute x1, starting transfers between devices, run(): lax.ppermute(lax.dynamic_slice_in_dim(queries[0], (1 - half) * width, wid...  6.03 us
    ppermute x1, starting transfers between devices, run(): other = lax.ppermute(theirs, first, swap)  3.32 us
  transfers between devices with their start and end apart: 2, of which 1 were waited for; matrix products, arithmetic and copies ran while one was open for 2% of the time, Pallas kernels for 3%

profile of v1, /device:TPU:80, one launch (start us, length us, event | category | flops | bytes accessed | tf_op | source)
XLA Modules:
  0.0 129.8 jit_solution(17747554155556932549)
XLA Ops:
  0.0 129.0 %conditional.1 = (bf16[1,64,4096]{2,1,0:T(8,128)(2,1)S(1)}) conditional(s32[]{:T(128)} %convert_element_type.49, (bf16[1,64,256]{2,1,0:T(8,128)(2,1)}, bf16[1,64,256]{2,1,0:T(8,128)(2,1)}, bf16[1,64,4096]{2,1,0:T(8,128)(2,1)}, s32[256]{0:T(256)}, s32[1]{0:T(128)}) %tuple.13, (bf16[1,64,256]{2,1,0:T(8,128)(2,1)}, bf16[1,64,256]{2,1,0:T(8,128)(2,1)}, ...), branch_computations={%region_0.1_spmd, %region_1.2_spmd} | conditional | flops 3604507 | bytes 20779424 | solution.py:223
  0.0 1.1 dynamic-slice_bitcast_fusion.5
  1.1 6.0 %collective-permute-start.2 = (bf16[64,2048]{1,0:T(8,128)(2,1)S(1)}, bf16[64,2048]{1,0:T(8,128)(2,1)S(1)}, u32[]{:S(2)}, u32[]{:S(2)}) collective-permute-start(bf16[64,2048]{1,0:T(8,128)(2,1)S(1)} %get-tuple-element.66), channel_id=1, source_target_pairs={{0,16},{16,0},{32,48},{48,32},{64,80},{80,64},{96,112},{112,96},{1... | collective-permute-start | bytes 786440 | tf_op jit(solution)/shard_map/cond/branch_1_fun/ppermute | solution.py:194
  7.1 0.8 slice_bitcast_fusion.6
  7.9 70.9 %all-gather.6 = f16[16,4,64,128]{3,2,1,0:T(8,128)(2,1)S(1)} all-gather(f16[1,4,64,128]{3,2,1,0:T(8,128)(2,1)S(1)} %multiply_convert_fusion.1), channel_id=1, replica_groups=mesh['rep'=2,'blk_0'=16,'blk_1'=8,'head'=2] {'blk_0'}, dimensions={0}, use_global_device_ids=true | all-gather | bytes 1114112 | tf_op jit(solution)/shard_map/cond/branch_1_fun/all_gather | solution.py:202
  78.8 0.2 dynamic-slice_bitcast_fusion.3
  79.0 33.5 %all-gather.7 = f16[128,2,64,128]{3,2,1,0:T(8,128)(2,1)S(1)} all-gather(f16[16,2,64,128]{3,2,1,0:T(8,128)(2,1)S(1)} %dynamic-slice_bitcast_fusion.3), channel_id=3, replica_groups=mesh['rep'=2,'blk_0'=16,'blk_1'=8,'head'=2] {'blk_1'}, dimensions={0}, use_global_device_ids=true | all-gather | bytes 4718592 | tf_op jit(solution)/shard_map/cond/branch_1_fun/all_gather | solution.py:208
  112.4 0.0 copy-start.2
  112.5 1.9 %convert_element_type.51 = bf16[128,2,64,128]{3,2,1,0:T(8,128)(2,1)S(1)} convert(f16[128,2,64,128]{3,2,1,0:T(8,128)(2,1)S(1)} %all-gather.7) | non-fusion elementwise | flops 2097152 | bytes 8388608 | tf_op jit(solution)/shard_map/cond/branch_1_fun/convert_element_type | solution.py:208
  114.4 0.0 collective-permute-done.2.refs_0_
  114.4 0.0 copy-done.2
  114.4 5.9 %branch_1_fun.2 = (bf16[64,2048]{1,0:T(8,128)(2,1)S(1)}, bf16[64,2048]{1,0:T(8,128)(2,1)S(1)}, bf16[512,32,128]{2,1,0:T(8,128)(2,1)S(1)}) custom-call(s32[256]{0:T(256)S(1)} %copy-done.2, s32[1]{0:T(128)} %get-tuple-element.45.length_ref, bf16[64,2048]{1,0:T(8,128)(2,1)S(1)} %collective-permute-done.2.refs_0_, ...), custom_call_target="tpu_custom_call", output_to_operand_aliasing={{2}: (4, {})} | custom-call | tf_op jit(solution)/shard_map/cond/branch_1_fun/pallas_call | solution.py:165
  120.3 3.3 %collective-permute-start.3 = (bf16[64,2048]{1,0:T(8,128)(2,1)S(1)}, bf16[64,2048]{1,0:T(8,128)(2,1)S(1)}, u32[]{:S(2)}, u32[]{:S(2)}) collective-permute-start(bf16[64,2048]{1,0:T(8,128)(2,1)S(1)} %get-tuple-element.51), channel_id=1, source_target_pairs={{0,16},{16,0},{32,48},{48,32},{64,80},{80,64},{96,112},{112,96},{1... | collective-permute-start | bytes 786440 | tf_op jit(solution)/shard_map/cond/branch_1_fun/ppermute | solution.py:213
  123.7 3.8 %branch_1_fun.3 = (bf16[64,2048]{1,0:T(8,128)(2,1)S(1)}, bf16[512,32,128]{2,1,0:T(8,128)(2,1)S(1)}) custom-call(s32[256]{0:T(256)S(1)} %copy-done.2, s32[1]{0:T(128)} %get-tuple-element.45.length_ref, bf16[64,2048]{1,0:T(8,128)(2,1)S(1)} %get-tuple-element.46.refs_1_.refs_0_, ...), custom_call_target="tpu_custom_call", output_to_operand_aliasing={{1}: (3, {}), {0}: (4, {})} | custom-call | tf_op jit(solution)/shard_map/cond/branch_1_fun/pallas_call | solution.py:165
  127.5 1.1 collective-permute-done.3
  129.0 0.0 copy-start
  129.0 0.8 copy-done
  (3 shorter events, 0.1 us)
Async XLA Ops:
  1.1 113.3 %collective-permute-start.2 = (bf16[64,2048]{1,0:T(8,128)(2,1)S(1)}, bf16[64,2048]{1,0:T(8,128)(2,1)S(1)}, u32[]{:S(2)}, u32[]{:S(2)}) collective-permute-start(bf16[64,2048]{1,0:T(8,128)(2,1)S(1)} %get-tuple-element.66), channel_id=1, source_target_pairs={{0,16},{16,0},{32,48},{48,32},{64,80},{80,64},{96,112},{112,96},{1... | collective-permute-start | bytes 786440 | tf_op jit(solution)/shard_map/cond/branch_1_fun/ppermute | solution.py:194
  112.4 2.0 %copy-start.2 = (s32[256]{0:T(256)S(1)}, s32[256]{0:T(256)}, u32[]{:S(2)}) copy-start(s32[256]{0:T(256)} %get-tuple-element.44.order_ref) | copy-start | bytes 3076 | tf_op jit(solution)/shard_map/cond
  120.3 8.3 %collective-permute-start.3 = (bf16[64,2048]{1,0:T(8,128)(2,1)S(1)}, bf16[64,2048]{1,0:T(8,128)(2,1)S(1)}, u32[]{:S(2)}, u32[]{:S(2)}) collective-permute-start(bf16[64,2048]{1,0:T(8,128)(2,1)S(1)} %get-tuple-element.51), channel_id=1, source_target_pairs={{0,16},{16,0},{32,48},{48,32},{64,80},{80,64},{96,112},{112,96},{1... | collective-permute-start | bytes 786440 | tf_op jit(solution)/shard_map/cond/branch_1_fun/ppermute | solution.py:213
  129.0 0.8 copy-start

commit v2 on v1

--- a/solution.py
+++ b/solution.py
@@ -8,8 +8,8 @@
 
 HEAD_WIDTH = 128
 BLK = ("blk_0", "blk_1")
-BLOCK_SPANS = 16
-STEP_BLOCKS = (8, 4, 2, 1)
+BLOCK_SPANS = 8
+STEP_BLOCKS = (16, 8, 4, 2, 1)
 NEG_FILL = -1e30
 LOG2_E = 1.4426950408889634
 SENT_SCALE = 4096.0

time: 132 us -> 139 us (1.053)
  Pallas kernels: 9.72 us -> 17.7 us
    pallas_call x2, Pallas kernels: 9.72 us -> 17.7 us  [attend(): pl.pallas_call(kernel, out_shape=(rows_shape,) * len(rows_of) + (jax.Shap...]
  transfers between devices with their start and end apart: 2 -> 2, of which waited for: 1 -> 0; matrix products, arithmetic and copies ran while one was open for 2% -> 2% of each run, Pallas kernels for 3% -> 7%
where the time goes in v2:
time: 139 us; the launch traced here: 137 us
  blocking collectives  104 us (75%)
  Pallas kernels  17.7 us (13%)
  starting transfers between devices  9.4 us (7%)
  local copies, waits for them, and re-layouts  2.8 us (2%)
  other arithmetic  2.05 us (1%)
    all_gather x1, blocking collectives, run(): part = lax.all_gather(packed, first, axis=0, tiled=False)  70.9 us
    all_gather x1, blocking collectives, run(): lax.all_gather(part, then, axis=0, tiled=False).astype(jnp.bfloat16)  33.5 us
    pallas_call x2, Pallas kernels, attend(): pl.pallas_call(kernel, out_shape=(rows_shape,) * len(rows_of) + (jax.Shap...  17.7 us
    ppermute x1, starting transfers between devices, run(): lax.ppermute(lax.dynamic_slice_in_dim(queries[0], (1 - half) * width, wid...  6.03 us
    ppermute x1, starting transfers between devices, run(): other = lax.ppermute(theirs, first, swap)  3.37 us
  transfers between devices with their start and end apart: 2, of which 0 were waited for; matrix products, arithmetic and copies ran while one was open for 2% of the time, Pallas kernels for 7%

profile of v2, /device:TPU:80, one launch (start us, length us, event | category | flops | bytes accessed | tf_op | source)
XLA Modules:
  0.0 136.7 jit_solution(14714335112578728525)
XLA Ops:
  0.0 135.9 %conditional.1 = (bf16[1,64,4096]{2,1,0:T(8,128)(2,1)S(1)}) conditional(s32[]{:T(128)} %convert_element_type.49, (bf16[1,64,256]{2,1,0:T(8,128)(2,1)}, bf16[1,64,256]{2,1,0:T(8,128)(2,1)}, bf16[1,64,4096]{2,1,0:T(8,128)(2,1)}, s32[256]{0:T(256)}, s32[1]{0:T(128)}) %tuple.13, (bf16[1,64,256]{2,1,0:T(8,128)(2,1)}, bf16[1,64,256]{2,1,0:T(8,128)(2,1)}, ...), branch_computations={%region_0.1_spmd, %region_1.2_spmd} | conditional | flops 3604507 | bytes 20779424 | solution.py:223
  0.0 1.1 dynamic-slice_bitcast_fusion.5
  1.1 6.0 %collective-permute-start.2 = (bf16[64,2048]{1,0:T(8,128)(2,1)S(1)}, bf16[64,2048]{1,0:T(8,128)(2,1)S(1)}, u32[]{:S(2)}, u32[]{:S(2)}) collective-permute-start(bf16[64,2048]{1,0:T(8,128)(2,1)S(1)} %get-tuple-element.66), channel_id=1, source_target_pairs={{0,16},{16,0},{32,48},{48,32},{64,80},{80,64},{96,112},{112,96},{1... | collective-permute-start | bytes 786440 | tf_op jit(solution)/shard_map/cond/branch_1_fun/ppermute | solution.py:194
  7.1 0.8 slice_bitcast_fusion.6
  7.9 70.9 %all-gather.6 = f16[16,4,64,128]{3,2,1,0:T(8,128)(2,1)S(1)} all-gather(f16[1,4,64,128]{3,2,1,0:T(8,128)(2,1)S(1)} %multiply_convert_fusion.1), channel_id=1, replica_groups=mesh['rep'=2,'blk_0'=16,'blk_1'=8,'head'=2] {'blk_0'}, dimensions={0}, use_global_device_ids=true | all-gather | bytes 1114112 | tf_op jit(solution)/shard_map/cond/branch_1_fun/all_gather | solution.py:202
  78.8 0.2 dynamic-slice_bitcast_fusion.3
  79.0 33.5 %all-gather.7 = f16[128,2,64,128]{3,2,1,0:T(8,128)(2,1)S(1)} all-gather(f16[16,2,64,128]{3,2,1,0:T(8,128)(2,1)S(1)} %dynamic-slice_bitcast_fusion.3), channel_id=3, replica_groups=mesh['rep'=2,'blk_0'=16,'blk_1'=8,'head'=2] {'blk_1'}, dimensions={0}, use_global_device_ids=true | all-gather | bytes 4718592 | tf_op jit(solution)/shard_map/cond/branch_1_fun/all_gather | solution.py:208
  112.4 0.0 copy-start.2
  112.5 1.9 %convert_element_type.51 = bf16[128,2,64,128]{3,2,1,0:T(8,128)(2,1)S(1)} convert(f16[128,2,64,128]{3,2,1,0:T(8,128)(2,1)S(1)} %all-gather.7) | non-fusion elementwise | flops 2097152 | bytes 8388608 | tf_op jit(solution)/shard_map/cond/branch_1_fun/convert_element_type | solution.py:208
  114.4 0.0 collective-permute-done.2.refs_0_
  114.4 0.0 copy-done.2
  114.4 8.4 %branch_1_fun.2 = (bf16[64,2048]{1,0:T(8,128)(2,1)S(1)}, bf16[64,2048]{1,0:T(8,128)(2,1)S(1)}, bf16[512,32,128]{2,1,0:T(8,128)(2,1)S(1)}) custom-call(s32[256]{0:T(256)S(1)} %copy-done.2, s32[1]{0:T(128)} %get-tuple-element.45.length_ref, bf16[64,2048]{1,0:T(8,128)(2,1)S(1)} %collective-permute-done.2.refs_0_, ...), custom_call_target="tpu_custom_call", output_to_operand_aliasing={{2}: (4, {})} | custom-call | tf_op jit(solution)/shard_map/cond/branch_1_fun/pallas_call | solution.py:165
  122.8 3.4 %collective-permute-start.3 = (bf16[64,2048]{1,0:T(8,128)(2,1)S(1)}, bf16[64,2048]{1,0:T(8,128)(2,1)S(1)}, u32[]{:S(2)}, u32[]{:S(2)}) collective-permute-start(bf16[64,2048]{1,0:T(8,128)(2,1)S(1)} %get-tuple-element.51), channel_id=1, source_target_pairs={{0,16},{16,0},{32,48},{48,32},{64,80},{80,64},{96,112},{112,96},{1... | collective-permute-start | bytes 786440 | tf_op jit(solution)/shard_map/cond/branch_1_fun/ppermute | solution.py:213
  126.2 9.3 %branch_1_fun.3 = (bf16[64,2048]{1,0:T(8,128)(2,1)S(1)}, bf16[512,32,128]{2,1,0:T(8,128)(2,1)S(1)}) custom-call(s32[256]{0:T(256)S(1)} %copy-done.2, s32[1]{0:T(128)} %get-tuple-element.45.length_ref, bf16[64,2048]{1,0:T(8,128)(2,1)S(1)} %get-tuple-element.46.refs_1_.refs_0_, ...), custom_call_target="tpu_custom_call", output_to_operand_aliasing={{1}: (3, {}), {0}: (4, {})} | custom-call | tf_op jit(solution)/shard_map/cond/branch_1_fun/pallas_call | solution.py:165
  135.5 0.0 collective-permute-done.3
  135.9 0.0 copy-start
  135.9 0.8 copy-done
  (3 shorter events, 0.1 us)
Async XLA Ops:
  1.1 113.3 %collective-permute-start.2 = (bf16[64,2048]{1,0:T(8,128)(2,1)S(1)}, bf16[64,2048]{1,0:T(8,128)(2,1)S(1)}, u32[]{:S(2)}, u32[]{:S(2)}) collective-permute-start(bf16[64,2048]{1,0:T(8,128)(2,1)S(1)} %get-tuple-element.66), channel_id=1, source_target_pairs={{0,16},{16,0},{32,48},{48,32},{64,80},{80,64},{96,112},{112,96},{1... | collective-permute-start | bytes 786440 | tf_op jit(solution)/shard_map/cond/branch_1_fun/ppermute | solution.py:194
  112.4 2.0 %copy-start.2 = (s32[256]{0:T(256)S(1)}, s32[256]{0:T(256)}, u32[]{:S(2)}) copy-start(s32[256]{0:T(256)} %get-tuple-element.44.order_ref) | copy-start | bytes 3076 | tf_op jit(solution)/shard_map/cond
  122.8 12.7 %collective-permute-start.3 = (bf16[64,2048]{1,0:T(8,128)(2,1)S(1)}, bf16[64,2048]{1,0:T(8,128)(2,1)S(1)}, u32[]{:S(2)}, u32[]{:S(2)}) collective-permute-start(bf16[64,2048]{1,0:T(8,128)(2,1)S(1)} %get-tuple-element.51), channel_id=1, source_target_pairs={{0,16},{16,0},{32,48},{48,32},{64,80},{80,64},{96,112},{112,96},{1... | collective-permute-start | bytes 786440 | tf_op jit(solution)/shard_map/cond/branch_1_fun/ppermute | solution.py:213
  135.9 0.8 copy-start
